TPU v7x, 256 devices: a whole 4x4x8 slice. The times are simulated.
256 devices in a mesh: dp: 8 (over z_hi, y), expert: 32 (over z_lo, x, core).
Axes of the slice: x: 4, y: 4, z: 8 (z_hi: 2, z_lo: 4; z = z_hi * 4 + z_lo), core: 2. Of those that a mesh axis runs over, the one named last changes fastest.
Arguments:
- routed: bfloat16 [32768, 7168], P(('dp', 'expert')), may hold values from -160 to 160
- expert_ids: int32 [32768, 8], P(('dp', 'expert')), may hold values from 0 to 255, all different within a row
- norm_gain: bfloat16 [7168], replicated, may hold values from 0.099609375 to 1.8984375
- gate_weight: bfloat16 [32, 7168, 2048], P('expert', None, 'dp'), may hold values from -0.0625 to 0.0625
- up_weight: bfloat16 [32, 7168, 2048], P('expert', None, 'dp'), may hold values from -0.0625 to 0.0625
- down_weight: bfloat16 [32, 2048, 7168], P('expert', 'dp'), may hold values from -0.125 to 0.125
- old_place: int32 [32], replicated, may hold values from 0 to 255, as said below
- new_place: int32 [32], replicated, may hold values from 0 to 255, as said below
- probe_ids: int32 [10240], P(('dp', 'expert')), may hold values from 0 to 127
Outputs:
- expert_load: float32 [256], P('expert')
- expert_energy: float32 [256], P('expert')
- probe_out: bfloat16 [10240, 7168], P(('dp', 'expert'))
Inputs may be any that keep to these rules, and one draw needn't show every extreme that they name: `old_place`: 32 different experts. `new_place`: the same 32 experts as old_place, in some order.
All inputs are finite; a program needn't handle non-finite values.
Results may differ from a plain program's by a relative error of at most 0.012.
Values may be sent and summed in bfloat16 or wider, within the bound.
A program may use at most 128 MiB of HBM per device.

v0:
```python
import math

import jax
import jax.numpy as jnp
from jax import lax
from jax.sharding import Mesh
from jax.sharding import PartitionSpec as P

EXP_DEV = 8
TOP = 8
DP = ("dp_0", "dp_1")
DP_EXPERT = ("dp_0", "dp_1", "expert")


epsilon = 1e-06


def own_block(blocks, axes, turns):
    inside = blocks.shape[1:]
    blocks = blocks.reshape(*(lax.axis_size(a) for a in axes), *inside)
    blocks = jnp.moveaxis(blocks, turns, range(len(axes))).reshape(-1, *inside)
    for k in turns:
        blocks = lax.psum_scatter(blocks, axes[k], scatter_dimension=0, tiled=True)
    return blocks[0]


def cut_along(value, dim, size):
    shape = value.shape
    blocks = value.reshape(*shape[:dim], size, shape[dim] // size, *shape[dim + 1 :])
    return jnp.moveaxis(blocks, dim, 0)


def sum_by_axis(value, axes, turns, dim):
    size = lax.axis_size(axes)
    return own_block(cut_along(value, dim, size), axes, turns)


def summed_on_arrival(value, axis, dim):
    blocks = cut_along(value, dim, lax.axis_size(axis))
    arrived = lax.all_to_all(blocks, axis, split_axis=0, concat_axis=0, tiled=True)
    return arrived.sum(axis=0)


def from_everyone(value, axis):
    copies = jnp.broadcast_to(value, (lax.axis_size(axis), *value.shape))
    return lax.all_to_all(copies, axis, split_axis=0, concat_axis=0, tiled=True)


def over_copies(value, axis):
    return from_everyone(value, axis).sum(axis=0)


def flatten_blocks(array, slots):
    length = array.size // slots
    lanes = math.gcd(length, 128)
    return array.reshape(slots, length // lanes, lanes)


def relay_rows(array, sources):
    shaped = flatten_blocks(array, sources.shape[0])
    moved = lax.all_to_all(
        jnp.take(
            lax.all_to_all(shaped, "expert", split_axis=0, concat_axis=0, tiled=True),
            sources,
            axis=0,
        ),
        "expert",
        split_axis=0,
        concat_axis=0,
        tiled=True,
    )
    return moved.reshape(array.shape)


def expert_block(normed, gate_matrix, up_matrix, down_matrix):
    piece = lax.all_gather(normed, DP, axis=0, tiled=True)
    gate_value = jnp.dot(piece, gate_matrix, preferred_element_type=jnp.float32)
    up_value = jnp.dot(piece, up_matrix, preferred_element_type=jnp.float32)
    hidden = (jax.nn.silu(gate_value) * up_value).astype(jnp.bfloat16)
    partial_sums = jnp.dot(hidden, down_matrix, preferred_element_type=jnp.float32)
    return (
        sum_by_axis(partial_sums.astype(jnp.bfloat16), DP, (1, 0), 0)
        .astype(jnp.float32)
        .astype(jnp.bfloat16)
    )


def on_device(
    routed,
    expert_ids,
    norm_gain,
    gate_weight,
    up_weight,
    down_weight,
    old_place,
    new_place,
    probe_ids,
):
    slots = lax.axis_size("expert")
    experts = EXP_DEV * slots
    tokens = routed.shape[0] * lax.axis_size(DP) * slots
    features = routed.astype(jnp.float32)
    mean_square = jnp.sum(features * features, axis=1) / routed.shape[1]
    positions = jnp.arange(experts, dtype=jnp.int32)
    onehot = jnp.sum(
        (expert_ids[:, :, None] == positions[None, None, :]).astype(jnp.float32), axis=1
    )
    columns = jnp.stack([jnp.ones_like(mean_square), mean_square])
    local_stats = jnp.dot(columns, onehot)
    owned = summed_on_arrival(local_stats, "expert", 1)
    owned = over_copies(owned, DP)
    expert_load = owned[0] * experts / (tokens * TOP)
    expert_energy = owned[1] / owned[0]
    picked_rows = jnp.take(routed, probe_ids, axis=0).astype(jnp.float32)
    scale = lax.rsqrt(jnp.take(mean_square, probe_ids) + epsilon)
    normed = (picked_rows * scale[:, None] * norm_gain.astype(jnp.float32)[None, :]).astype(
        jnp.bfloat16
    )
    slot_index = jnp.arange(slots, dtype=jnp.int32)
    matches = new_place[:, None] == old_place[None, :]
    sources = jnp.sum(jnp.where(matches, slot_index[None, :], 0), axis=1)
    targets = jnp.sum(jnp.where(matches, slot_index[:, None], 0), axis=0)
    arrived = relay_rows(normed, targets)
    computed = expert_block(arrived, gate_weight[0], up_weight[0], down_weight[0])
    probe_out = relay_rows(computed, sources)
    return (expert_load, expert_energy, probe_out)


def solution(mesh):
    split = Mesh(mesh.devices.reshape(2, 4, mesh.shape["expert"]), ("dp_0", "dp_1", "expert"))
    return jax.shard_map(
        on_device,
        mesh=split,
        in_specs=(
            P(DP_EXPERT, None),
            P(DP_EXPERT, None),
            P(),
            P("expert", None, DP),
            P("expert", None, DP),
            P("expert", DP, None),
            P(),
            P(),
            P(DP_EXPERT),
        ),
        out_specs=(P("expert"), P("expert"), P(DP_EXPERT, None)),
        check_vma=False,
    )
```

profile of v0, /device:TPU:1, one launch (start us, length us, event | category | flops | bytes accessed | tf_op | source)
XLA Modules:
  0.0 354.8 jit_solution(17442525029706744475)
XLA Ops:
  7.2 0.8 compare_select_fusion.4
  8.0 1.9 multiply_reduce_fusion
  10.0 0.9 gather_fusion
  10.9 0.8 gather_fusion.1
  12.0 0.8 gather.14
  13.1 1.5 multiply_convert_fusion
  14.6 10.0 %all-to-all-start.2 = ((bf16[32,70,128]{2,1,0:T(8,128)(2,1)}), bf16[32,70,128]{2,1,0:T(8,128)(2,1)S(1)}, u32[]{:S(2)}, u32[]{:S(2)}) async-start(bf16[32,70,128]{2,1,0:T(8,128)(2,1)} %multiply_convert_fusion), calls=%async_computation.2 | async-start | bytes 1179648 | tf_op jit(solution)/shard_map/all_to_all | solution.py:63
  24.9 17.5 %all-to-all-done.2 = bf16[32,70,128]{2,1,0:T(8,128)(2,1)S(1)} async-done(((bf16[32,70,128]{2,1,0:T(8,128)(2,1)}), bf16[32,70,128]{2,1,0:T(8,128)(2,1)S(1)}, u32[]{:S(2)}, u32[]{:S(2)}) %all-to-all-start.2) | async-done | bytes 573472 | tf_op jit(solution)/shard_map/all_to_all | solution.py:63
  42.4 0.7 gather_fusion.2
  43.2 21.7 %all_to_all.30 = bf16[32,70,128]{2,1,0:T(8,128)(2,1)S(1)} all-to-all(bf16[32,70,128]{2,1,0:T(8,128)(2,1)S(1)} %broadcast_select_fusion.1), channel_id=1, replica_groups=mesh['dp_0'=2,'dp_1'=4,'expert'=32] {'expert'}, dimensions={0} | all-to-all | bytes 1146880 | tf_op jit(solution)/shard_map/all_to_all | solution.py:61
  64.9 1.5 reshape.57
  66.4 103.2 %all-gather.2.cloned.1.call-done = bf16[320,7168]{1,0:T(8,128)(2,1)} async-done(((bf16[40,7168]{1,0:T(8,128)(2,1)}), bf16[320,7168]{1,0:T(8,128)(2,1)}) %all-gather.2.cloned.1.call-update) | async-done | bytes 4587536 | tf_op jit(solution)/shard_map/all_gather | solution.py:76
  169.6 4.9 %fusion.3 = f32[320,256]{1,0:T(8,128)S(1)} fusion(bf16[320,7168]{1,0:T(8,128)(2,1)} %all-gather.2.cloned.1.call-done, bf16[1,7168,256]{2,1,0:T(8,128)(2,1)} %param.14), kind=kOutput, calls=%fused_computation.8 | convolution fusion | flops 1174405120 | bytes 8585216 | tf_op jit(solution)/shard_map/dot_general | solution.py:77
  174.5 0.9 copy-done.8
  175.4 1.4 fusion.8
  176.8 0.6 copy-done.1
  177.5 1.4 convolution_convert_fusion
  178.8 2.5 copy.42
  181.4 55.7 %reduce-scatter.3.cloned.1.call-done = bf16[2,40,7168]{2,1,0:T(8,128)(2,1)} async-done(((bf16[8,40,7168]{2,1,0:T(8,128)(2,1)}), bf16[2,40,7168]{2,1,0:T(8,128)(2,1)}) %reduce-scatter.3.cloned.1.call-update) | async-done | bytes 1146896 | tf_op jit(solution)/shard_map/reduce_scatter | solution.py:23
  237.9 0.7 copy.38
  238.7 8.1 %all-to-all-start = ((f32[32,2,8]{2,1,0:T(2,128)}), f32[32,2,8]{2,1,0:T(2,128)S(1)}, u32[]{:S(2)}, u32[]{:S(2)}) async-start(f32[32,2,8]{2,1,0:T(2,128)} %copy.38), calls=%async_computation | async-start | bytes 65536 | tf_op jit(solution)/shard_map/all_to_all | solution.py:40
  246.8 34.2 %reduce-scatter.5.cloned.1.call-done = bf16[1,40,7168]{2,1,0:T(8,128)(2,1)} async-done(((bf16[2,40,7168]{2,1,0:T(8,128)(2,1)}), bf16[1,40,7168]{2,1,0:T(8,128)(2,1)}) %reduce-scatter.5.cloned.1.call-update) | async-done | bytes 573456 | tf_op jit(solution)/shard_map/reduce_scatter | solution.py:23
  281.0 2.7 reshape.59
  283.6 6.8 %all-to-all-start.4 = ((bf16[32,70,128]{2,1,0:T(8,128)(2,1)}), bf16[32,70,128]{2,1,0:T(8,128)(2,1)S(1)}, u32[]{:S(2)}, u32[]{:S(2)}) async-start(bf16[32,70,128]{2,1,0:T(8,128)(2,1)} %reshape.59), calls=%async_computation.6 | async-start | bytes 1179648 | tf_op jit(solution)/shard_map/all_to_all | solution.py:63
  290.5 17.7 %all-to-all-done.4 = bf16[32,70,128]{2,1,0:T(8,128)(2,1)S(1)} async-done(((bf16[32,70,128]{2,1,0:T(8,128)(2,1)}), bf16[32,70,128]{2,1,0:T(8,128)(2,1)S(1)}, u32[]{:S(2)}, u32[]{:S(2)}) %all-to-all-start.4) | async-done | bytes 573472 | tf_op jit(solution)/shard_map/all_to_all | solution.py:63
  308.8 5.8 %all-to-all-start.1 = ((f32[8,2,8]{2,1,0:T(2,128)}), f32[8,2,8]{2,1,0:T(2,128)S(1)}, u32[]{:S(2)}, u32[]{:S(2)}) async-start(f32[8,2,8]{2,1,0:T(2,128)} %broadcast_in_dim.64), calls=%async_computation.1 | async-start | bytes 16384 | tf_op jit(solution)/shard_map/all_to_all | solution.py:46
  314.5 0.7 gather_fusion.3
  315.2 0.9 broadcast_select_fusion
  316.1 7.3 %all-to-all-done.1 = f32[8,2,8]{2,1,0:T(2,128)S(1)} async-done(((f32[8,2,8]{2,1,0:T(2,128)}), f32[8,2,8]{2,1,0:T(2,128)S(1)}, u32[]{:S(2)}, u32[]{:S(2)}) %all-to-all-start.1) | async-done | bytes 544 | tf_op jit(solution)/shard_map/all_to_all | solution.py:46
  323.5 5.6 %all-to-all-start.5 = ((bf16[32,70,128]{2,1,0:T(8,128)(2,1)}), bf16[32,70,128]{2,1,0:T(8,128)(2,1)S(1)}, u32[]{:S(2)}, u32[]{:S(2)}) async-start(bf16[32,70,128]{2,1,0:T(8,128)(2,1)} %broadcast_select_fusion), calls=%async_computation.7 | async-start | bytes 1179648 | tf_op jit(solution)/shard_map/all_to_all | solution.py:61
  329.6 17.2 %all-to-all-done.5 = bf16[32,70,128]{2,1,0:T(8,128)(2,1)S(1)} async-done(((bf16[32,70,128]{2,1,0:T(8,128)(2,1)}), bf16[32,70,128]{2,1,0:T(8,128)(2,1)S(1)}, u32[]{:S(2)}, u32[]{:S(2)}) %all-to-all-start.5) | async-done | bytes 573472 | tf_op jit(solution)/shard_map/all_to_all | solution.py:61
  346.8 1.5 reshape.60
  (49 shorter events, 3.1 us)
Async XLA Ops:
  7.2 2.8 copy-start
  8.0 3.7 %copy-start.4 = (s32[40]{0:T(128)S(1)}, s32[40]{0:T(128)}, u32[]{:S(2)}) copy-start(s32[40]{0:T(128)} %param.19) | copy-start | bytes 484
  9.9 2.9 copy-start.2
  12.8 11.9 %copy-start.5 = (s32[32]{0:T(128)S(1)}, s32[32]{0:T(128)}, u32[]{:S(2)}) copy-start(s32[32]{0:T(128)} %param.17) | copy-start | bytes 388
  12.8 11.9 %copy-start.6 = (s32[32]{0:T(128)S(1)}, s32[32]{0:T(128)}, u32[]{:S(2)}) copy-start(s32[32]{0:T(128)} %param.18) | copy-start | bytes 388
  14.6 27.8 %all-to-all-start.2 = ((bf16[32,70,128]{2,1,0:T(8,128)(2,1)}), bf16[32,70,128]{2,1,0:T(8,128)(2,1)S(1)}, u32[]{:S(2)}, u32[]{:S(2)}) async-start(bf16[32,70,128]{2,1,0:T(8,128)(2,1)} %multiply_convert_fusion), calls=%async_computation.2 | async-start | bytes 1179648 | tf_op jit(solution)/shard_map/all_to_all | solution.py:63
  24.6 144.9 %all-gather.2.cloned.1.call-start = ((), (), s32[]{:S(2)}) async-start(), calls=%async_computation.8 | async-start | bytes 5160960 | tf_op jit(solution)/shard_map/all_gather | solution.py:76
  66.4 170.7 %reduce-scatter.3.cloned.1.call-start = ((), (), s32[]{:S(2)}) async-start(), calls=%async_computation.9 | async-start | bytes 5734400 | tf_op jit(solution)/shard_map/reduce_scatter | solution.py:23
  169.6 4.9 %copy-start.7 = (bf16[320,7168]{1,0:T(8,128)(2,1)S(1)}, bf16[320,7168]{1,0:T(8,128)(2,1)}, u32[]{:S(2)}) copy-start(bf16[320,7168]{1,0:T(8,128)(2,1)} %all-gather.2.cloned.1.call-done) | copy-start | bytes 13762564
  169.6 5.9 %copy-start.8 = (bf16[1,7168,256]{2,1,0:T(8,128)(2,1)S(1)}, bf16[1,7168,256]{2,1,0:T(8,128)(2,1)}, u32[]{:S(2)}) copy-start(bf16[1,7168,256]{2,1,0:T(8,128)(2,1)} %param.15) | copy-start | bytes 11010052
  175.4 2.0 copy-start.1
  181.3 55.8 %copy-start.3 = (s32[128,8]{0,1:T(8,128)S(1)}, s32[128,8]{0,1:T(8,128)}, u32[]{:S(2)}) copy-start(s32[128,8]{0,1:T(8,128)} %param.12) | copy-start | bytes 12292
  181.3 99.6 %reduce-scatter.5.cloned.1.call-start = ((), (), s32[]{:S(2)}) async-start(), calls=%async_computation.10 | async-start | bytes 1720320 | tf_op jit(solution)/shard_map/reduce_scatter | solution.py:23
  238.7 44.9 %all-to-all-start = ((f32[32,2,8]{2,1,0:T(2,128)}), f32[32,2,8]{2,1,0:T(2,128)S(1)}, u32[]{:S(2)}, u32[]{:S(2)}) async-start(f32[32,2,8]{2,1,0:T(2,128)} %copy.38), calls=%async_computation | async-start | bytes 65536 | tf_op jit(solution)/shard_map/all_to_all | solution.py:40
  283.6 24.5 %all-to-all-start.4 = ((bf16[32,70,128]{2,1,0:T(8,128)(2,1)}), bf16[32,70,128]{2,1,0:T(8,128)(2,1)S(1)}, u32[]{:S(2)}, u32[]{:S(2)}) async-start(bf16[32,70,128]{2,1,0:T(8,128)(2,1)} %reshape.59), calls=%async_computation.6 | async-start | bytes 1179648 | tf_op jit(solution)/shard_map/all_to_all | solution.py:63
  308.8 14.7 %all-to-all-start.1 = ((f32[8,2,8]{2,1,0:T(2,128)}), f32[8,2,8]{2,1,0:T(2,128)S(1)}, u32[]{:S(2)}, u32[]{:S(2)}) async-start(f32[8,2,8]{2,1,0:T(2,128)} %broadcast_in_dim.64), calls=%async_computation.1 | async-start | bytes 16384 | tf_op jit(solution)/shard_map/all_to_all | solution.py:46
  323.5 23.4 %all-to-all-start.5 = ((bf16[32,70,128]{2,1,0:T(8,128)(2,1)}), bf16[32,70,128]{2,1,0:T(8,128)(2,1)S(1)}, u32[]{:S(2)}, u32[]{:S(2)}) async-start(bf16[32,70,128]{2,1,0:T(8,128)(2,1)} %broadcast_select_fusion), calls=%async_computation.7 | async-start | bytes 1179648 | tf_op jit(solution)/shard_map/all_to_all | solution.py:61
Sparse Core Ops, SparseCore 0:
  66.5 103.0 all-gather.1
  181.5 55.5 reduce-scatter.2
  239.6 41.2 reduce-scatter.4
where the time goes:
time: 355 us
  waiting for transfers between devices  253 us (71%)
  starting transfers between devices  36.4 us (10%)
  blocking collectives  21.7 us (6%)
  local copies, waits for them, and re-layouts  15.6 us (4%)
  between operations  14 us (4%)
  matrix products  7.84 us (2%)
  other arithmetic  6.51 us (2%)
    all_gather x1, waiting for transfers between devices, expert_block(): piece = lax.all_gather(normed, DP, axis=0, tiled=True)  103 us
    reduce_scatter x2, waiting for transfers between devices, own_block(): blocks = lax.psum_scatter(blocks, axes[k], scatter_dimension=0, tiled=True)  89.9 us
    all_to_all x2, waiting for transfers between devices, relay_rows(): lax.all_to_all(shaped, 'expert', split_axis=0, concat_axis=0, tiled=True)  35.1 us
    all_to_all x1, blocking collectives, relay_rows(): lax.all_to_all(jnp.take(lax.all_to_all(shaped, 'expert', split_axis=0, co...  21.7 us
    all_to_all x1, waiting for transfers between devices, relay_rows(): lax.all_to_all(jnp.take(lax.all_to_all(shaped, 'expert', split_axis=0, co...  17.2 us
    all_to_all x2, starting transfers between devices, relay_rows(): lax.all_to_all(shaped, 'expert', split_axis=0, concat_axis=0, tiled=True)  16.8 us
    all_to_all x1, starting transfers between devices, summed_on_arrival(): lax.all_to_all(blocks, axis, split_axis=0, concat_axis=0, tiled=True)  8.12 us
    all_to_all x1, waiting for transfers between devices, from_everyone(): return lax.all_to_all(copies, axis, split_axis=0, concat_axis=0, tiled=True)  7.34 us
  transfers between devices with their start and end apart: 8, of which 7 were waited for; matrix products, arithmetic and copies ran while one was open for 2% of the time, Pallas kernels for 0%

commit v1 on v0

v1 whole, which is shorter than its diff:
```python
import functools

import jax
import jax.numpy as jnp
from jax import lax
from jax.experimental import pallas as pl
from jax.experimental.pallas import tpu as pltpu
from jax.sharding import PartitionSpec as P

MESH = pl.DeviceIdType.MESH
F32 = jnp.float32
BF16 = jnp.bfloat16
EXP_DEV = 8
TOP = 8
EPS = 1e-06
PC = 256


class Layout:
    def __init__(self, zh=2, y=4, zl=4, x=4, c=2, pieces=7, rows=40, toks=128, hid=256):
        self.ZH, self.Y, self.ZL, self.X, self.C = zh, y, zl, x, c
        self.KP, self.ROWS, self.TOKS, self.HID = pieces, rows, toks, hid
        self.NZ, self.NXC = zh * zl, x * c
        self.NS = zl * x * c
        self.CW = pieces * PC
        self.D = zl * self.CW


def kernel(
    L, tokens,
    tgt_ref, src_ref, pid_ref, ids_ref, gain_ref, routed_hbm, gate_hbm, up_hbm, down_hbm,
    load_ref, energy_ref, out_hbm,
    routed_v, gain_v, gate_v, up_v, down_v,
    send1, recv1, send2, xbuf, gacc, uacc, hid,
    pbuf, ra, rb, bs, sz, zr, f1, fin,
    st_y, st_z, st_x, st_c,
    in_sem, w_sem, s1_send, s1_recv, s2_send, s2_recv, y_send, yp_recv, ym_recv, yf_recv,
    r_send, ra_recv, rb0_recv, rb1_recv, z_send, zr_recv, f_send, f_recv, st_send, st_recv,
):
    Y, ZL, X, C, KP, NZ, NXC, NS, CW = L.Y, L.ZL, L.X, L.C, L.KP, L.NZ, L.NXC, L.NS, L.CW
    rows = L.ROWS
    me_d, me_e = lax.axis_index("dp"), lax.axis_index("expert")
    zh, y = me_d // Y, me_d % Y
    zl, xc = me_e // NXC, me_e % NXC
    x, c = xc // C, xc % C
    p = zh * ZL + zl
    kme = (xc - C * zl + C * NXC) % NXC
    active = kme < KP
    mine = p * NXC + xc

    def dev(z, yy, xcc):
        return ((z // ZL) * Y + yy, (z % ZL) * NXC + xcc)

    def half(r, z_low):
        return ((r - z_low + ZL // 2 - 1 + r % 2 + NZ) % NZ) // ZL

    def cols(k):
        return pl.ds(pl.multiple_of(k * PC, PC), PC)

    def remote(src, dst, send, recv, where):
        pltpu.make_async_remote_copy(
            src_ref=src, dst_ref=dst, send_sem=send, recv_sem=recv, device_id=where, device_id_type=MESH
        ).start()

    def wait(ref, sem):
        pltpu.make_async_copy(ref, ref, sem).wait()

    copy_in = pltpu.make_async_copy(routed_hbm, routed_v, in_sem)
    copy_in.start()
    barrier = pltpu.get_barrier_semaphore()

    @pl.loop(0, NZ * NXC)
    def _(q):
        @pl.when(q != mine)
        def _():
            pl.semaphore_signal(barrier, inc=1, device_id=dev(q // NXC, y, q % NXC), device_id_type=MESH)

    for dy in range(1, Y):
        pl.semaphore_signal(barrier, inc=1, device_id=dev(p, (y + dy) % Y, xc), device_id_type=MESH)

    gain_v[...] = gain_ref[...].astype(F32)
    lane = lax.broadcasted_iota(jnp.int32, (8, L.TOKS), 1)
    sub = lax.broadcasted_iota(jnp.int32, (8, L.TOKS), 0)
    picks = []
    for b in range(rows // 8):
        want = jnp.zeros((8, L.TOKS), jnp.int32)
        for i in range(8):
            want = jnp.where(sub == i, pid_ref[b * 8 + i], want)
        picks.append((lane == want).astype(F32))
    select = jnp.concatenate(picks, axis=0).astype(BF16)

    copy_in.wait()
    for hbm, v in ((gate_hbm, gate_v), (up_hbm, up_v)):
        for m in range(ZL):
            pltpu.make_async_copy(hbm.at[pl.ds(m * CW, CW), :], v.at[m], w_sem).start()
    for m in range(ZL):
        pltpu.make_async_copy(down_hbm.at[:, pl.ds(m * CW, CW)], down_v.at[m], w_sem).start()

    square = jnp.zeros((rows, 1), F32)
    for m in range(ZL):
        picked = jnp.dot(select, routed_v[:, m * CW : (m + 1) * CW], preferred_element_type=F32)
        square += jnp.sum(picked * picked, axis=1, keepdims=True)
        send1[m] = picked.astype(BF16)
    scale = lax.rsqrt(square / L.D + EPS)
    for m in range(ZL):
        for t in range(CW // 128):
            tile = m * (CW // 128) + t
            v = send1[m, :, t * 128 : (t + 1) * 128].astype(F32)
            send1[m, :, t * 128 : (t + 1) * 128] = (v * scale * gain_v[tile : tile + 1, :]).astype(BF16)

    pl.semaphore_wait(barrier, NZ * NXC - 1 + Y - 1)

    @pl.loop(0, ZL * KP)
    def _(i):
        idx = (i + (xc % KP) * ZL + zl) % (ZL * KP)
        m, k = idx % ZL, idx // ZL
        r = m + ZL * ((half(m, zl) + zh) % 2)
        xct = (k + C * m) % NXC

        @pl.when(r * NXC + xct != mine)
        def _():
            remote(send1.at[m, :, cols(k)], recv1.at[me_e], s1_send, s1_recv, dev(r, y, xct))

    def squares(i, acc):
        v = routed_v[:, pl.ds(pl.multiple_of(i * PC, PC), PC)].astype(F32)
        return acc + v * v

    total = lax.fori_loop(0, L.D // PC, squares, jnp.zeros((L.TOKS, PC), F32))
    mean_square = jnp.sum(total, axis=1, keepdims=True) / L.D
    ids = ids_ref[...].astype(F32).T
    expert = lax.broadcasted_iota(jnp.int32, (L.TOKS, 256), 1).astype(F32)
    onehot = jnp.zeros((L.TOKS, 256), F32)
    for k in range(TOP):
        onehot += (ids[:, k : k + 1] == expert).astype(F32)
    counts = jnp.sum(onehot, axis=0, keepdims=True)
    energy = jnp.sum(onehot * mean_square, axis=0, keepdims=True)
    stats = jnp.concatenate(
        [counts[:, :128], counts[:, 128:], energy[:, :128], energy[:, 128:], jnp.zeros((4, 128), F32)], axis=0
    )
    rounds = (
        (st_y, Y, y, lambda o: dev(p, o, xc)),
        (st_z, NZ, p, lambda o: dev(o, y, xc)),
        (st_x, X, x, lambda o: dev(p, y, o * C + c)),
        (st_c, C, c, lambda o: dev(p, y, x * C + o)),
    )

    def stats_store(n, value):
        buf, _, own, _ = rounds[n]
        buf[own] = value

    def stats_send(n):
        buf, size, own, where = rounds[n]
        for step in range(1, size):
            remote(buf.at[own], buf.at[own], st_send.at[n], st_recv.at[n], where((own + step) % size))

    def stats_sum(n):
        buf, size, own, _ = rounds[n]
        if size > 1:
            wait(buf.at[pl.ds(0, size - 1)], st_recv.at[n])
            wait(buf.at[pl.ds(0, size - 1)], st_send.at[n])
        value = buf[0]
        for o in range(1, size):
            value += buf[o]
        return value

    def stats_out(value):
        ratio = value[2:4, :] / value[0:2, :]
        load = value[0:2, :] * (EXP_DEV * NS / (tokens * TOP))
        where = lax.broadcasted_iota(jnp.int32, (2, 128), 0) * 128 + lax.broadcasted_iota(jnp.int32, (2, 128), 1)
        for i in range(EXP_DEV):
            hit = where == me_e * EXP_DEV + i
            load_ref[i] = jnp.sum(jnp.where(hit, load, 0.0))
            energy_ref[i] = jnp.sum(jnp.where(hit, ratio, 0.0))

    tasks = [lambda: stats_store(0, stats), lambda: stats_send(0)]
    for n in range(1, 4):
        tasks.append(functools.partial(lambda n: stats_store(n, stats_sum(n - 1)), n))
        tasks.append(functools.partial(stats_send, n))
    tasks.append(lambda: stats_out(stats_sum(3)))

    def next_task():
        if tasks:
            tasks.pop(0)()

    next_task()

    @pl.when(active)
    def _():
        recv1[me_e] = send1[zl, :, cols(kme)]
        wait(recv1.at[pl.ds(0, NS - 1)], s1_recv)

        @pl.loop(0, NS)
        def _(j):
            send2[j] = recv1[tgt_ref[j]]

        xbuf[p, y, :, cols(kme)] = recv1[tgt_ref[me_e]]

        @pl.loop(1, NZ * NXC)
        def _(q):
            t = q // NXC
            z = (p + ((t + 1) // 2) * (2 * (t % 2) - 1) + NZ) % NZ
            xct = (xc + q) % NXC
            remote(
                send2.at[(z % ZL) * NXC + xct], xbuf.at[p, y, :, cols(kme)], s2_send, s2_recv.at[p], dev(z, y, xct)
            )

    offs = [((t + 1) // 2) * (2 * (t % 2) - 1) for t in range(NZ)]
    slot = tgt_ref[me_e]
    slot_z = slot // NXC
    ynext, yprev, yopp = (y + 1) % Y, (y + Y - 1) % Y, (y + 2) % Y

    def ring(i):
        return (p + offs[i] + NZ) % NZ

    def own_group(i):
        r = ring(i)
        if offs[i] == 0:
            @pl.when(active)
            def _():
                if KP > 1:
                    wait(xbuf.at[r, y, :, pl.ds(0, CW - PC)], s2_recv.at[r])

            @pl.when(jnp.logical_not(active))
            def _():
                wait(xbuf.at[r, y], s2_recv.at[r])
        else:
            wait(xbuf.at[r, y], s2_recv.at[r])
        remote(xbuf.at[r, y], xbuf.at[r, y], y_send, yp_recv.at[i], dev(p, ynext, xc))
        remote(xbuf.at[r, y], xbuf.at[r, y], y_send, ym_recv.at[i], dev(p, yprev, xc))

    def forward(i):
        r = ring(i)
        if i % 2 == 0:
            wait(xbuf.at[r, yprev], yp_recv.at[i])
            remote(xbuf.at[r, yprev], xbuf.at[r, yprev], y_send, yf_recv.at[i], dev(p, ynext, xc))
        else:
            wait(xbuf.at[r, ynext], ym_recv.at[i])
            remote(xbuf.at[r, ynext], xbuf.at[r, ynext], y_send, yf_recv.at[i], dev(p, yprev, xc))

    def arrived(i):
        r = ring(i)
        if i % 2 == 0:
            wait(xbuf.at[r, ynext], ym_recv.at[i])
        else:
            wait(xbuf.at[r, yprev], yp_recv.at[i])
        wait(xbuf.at[r, yopp], yf_recv.at[i])

    pairs = []
    for a in range(NZ):
        for b in range(a + 1, NZ):
            if (offs[a] - offs[b]) % NZ == ZL:
                pairs.append((b, a))
    pairs.sort()
    first = [True]

    def project(a, b):
        arrived(a)
        arrived(b)
        m = ring(a) % ZL
        near = half(m, slot_z) == 0
        lhs = jnp.concatenate([xbuf[m].reshape(Y * rows, CW), xbuf[m + ZL].reshape(Y * rows, CW)], axis=0)
        opening = first[0]
        first[0] = False
        if opening:
            wait(gate_v, w_sem)
            wait(up_v, w_sem)
            wait(down_v, w_sem)
        for weight, acc in ((gate_v, gacc), (up_v, uacc)):
            value = jnp.dot(lhs, weight[m], preferred_element_type=F32)
            a, b = value[: Y * rows], value[Y * rows :]
            for h, part in ((0, jnp.where(near, a, b)), (1, jnp.where(near, b, a))):
                if opening:
                    acc[h] = part
                else:
                    acc[h] += part

    for i in range(NZ):
        own_group(i)
        if i >= 1:
            forward(i - 1)
            next_task()
        if pairs and pairs[0][0] + 2 <= i:
            b, a = pairs.pop(0)
            project(a, b)
    forward(NZ - 1)
    for b, a in pairs:
        project(a, b)

    g = gacc[...]
    hid[...] = (g / (1.0 + jnp.exp(-g)) * uacc[...]).astype(BF16)

    def back(i):
        return ring(NZ - 1 - i)

    def sign(i):
        return (ynext, yprev) if i % 2 == 0 else (yprev, ynext)

    def compute(i):
        r = back(i)
        value = jnp.dot(hid[half(r, slot_z)], down_v[r % ZL], preferred_element_type=F32)
        pbuf[i] = value.astype(BF16).reshape(Y, rows, CW)

    def send_parts(i):
        to, other = sign(i)
        remote(pbuf.at[i, yopp], ra.at[i], r_send, ra_recv.at[i], dev(p, to, xc))
        remote(pbuf.at[i, other], rb.at[i, 0], r_send, rb0_recv.at[i], dev(p, other, xc))

    def add_passing(i):
        to, _ = sign(i)
        wait(ra.at[i], ra_recv.at[i])
        bs[i] = (pbuf[i, to].astype(F32) + ra[i].astype(F32)).astype(BF16)

    def send_passing(i):
        to, _ = sign(i)
        remote(bs.at[i], rb.at[i, 1], r_send, rb1_recv.at[i], dev(p, to, xc))

    def add_own(i):
        wait(rb.at[i, 0], rb0_recv.at[i])
        wait(rb.at[i, 1], rb1_recv.at[i])
        sz[i] = (pbuf[i, y].astype(F32) + rb[i, 0].astype(F32) + rb[i, 1].astype(F32)).astype(BF16)

    def send_relays(i):
        r = back(i)
        m = r % ZL
        mine_here = offs[NZ - 1 - i] == 0

        @pl.loop(0, KP)
        def _(kk):
            k = (kk + xc) % KP
            xct = (k + C * m) % NXC

            def go():
                remote(sz.at[i, :, cols(k)], zr.at[mine], z_send, zr_recv, dev(r, y, xct))

            if mine_here:
                pl.when(xct != xc)(go)
            else:
                go()

    compute(0)
    for i in range(NZ + 2):
        if i + 1 < NZ:
            compute(i + 1)
        if i < NZ:
            send_parts(i)
        if 1 <= i <= NZ:
            add_passing(i - 1)
        if i >= 2:
            add_own(i - 2)
        if 1 <= i <= NZ:
            send_passing(i - 1)
        next_task()
        if i >= 2:
            send_relays(i - 2)
    while tasks:
        next_task()

    @pl.when(active)
    def _():
        zr[mine] = sz[NZ - 1, :, cols(kme)]
        wait(zr.at[pl.ds(0, NZ * NXC - 1)], zr_recv)

        @pl.loop(0, NS)
        def _(s):
            j = src_ref[s]
            f1[s] = (zr[j].astype(F32) + zr[j + NS].astype(F32)).astype(BF16)

        fin[:, pl.ds(pl.multiple_of(zl * CW + kme * PC, PC), PC)] = f1[me_e]

        @pl.loop(1, NS)
        def _(i):
            s = (me_e + i) % NS
            s_z = s // NXC
            remote(
                f1.at[s],
                fin.at[:, pl.ds(pl.multiple_of(zl * CW + kme * PC, PC), PC)],
                f_send,
                f_recv,
                dev(ZL * half(p, s_z) + s_z, y, s % NXC),
            )

        wait(send2.at[pl.ds(0, ZL * KP - 1)], f_recv)

    @pl.when(jnp.logical_not(active))
    def _():
        wait(fin, f_recv)

    copy_out = pltpu.make_async_copy(fin, out_hbm, in_sem)
    copy_out.start()

    @pl.when(active)
    def _():
        wait(zr.at[pl.ds(0, ZL * KP - 1)], s1_send)
        wait(zr.at[pl.ds(0, NZ * NXC - 1)], s2_send)
        wait(zr.at[pl.ds(0, NZ * KP - 1)], z_send)
        wait(zr.at[pl.ds(0, NS - 1)], f_send)

    @pl.when(jnp.logical_not(active))
    def _():
        wait(zr.at[pl.ds(0, ZL * KP)], s1_send)
        wait(zr.at[pl.ds(0, NZ * KP)], z_send)

    wait(pbuf.at[pl.ds(0, 3 * NZ // Y)], y_send)
    wait(pbuf.at[pl.ds(0, 3 * NZ // Y)], r_send)
    copy_out.wait()


def on_device(L, tokens, routed, expert_ids, norm_gain, gate_weight, up_weight, down_weight, old_place, new_place, probe_ids):
    slot_index = jnp.arange(L.NS, dtype=jnp.int32)
    matches = new_place[:, None] == old_place[None, :]
    sources = jnp.sum(jnp.where(matches, slot_index[None, :], 0), axis=1)
    targets = jnp.sum(jnp.where(matches, slot_index[:, None], 0), axis=0)
    NZ, NXC, Y, ZL, KP, NS, CW, rows = L.NZ, L.NXC, L.Y, L.ZL, L.KP, L.NS, L.CW, L.ROWS
    smem = pl.BlockSpec(memory_space=pltpu.SMEM)
    vmem = pl.BlockSpec(memory_space=pltpu.VMEM)
    anyspace = pl.BlockSpec(memory_space=pl.ANY)
    dma = pltpu.SemaphoreType.DMA
    V = pltpu.VMEM
    scratch = [
        V((L.TOKS, L.D), BF16), V((L.D // 128, 128), F32),
        V((ZL, CW, L.HID), BF16), V((ZL, CW, L.HID), BF16), V((ZL, L.HID, CW), BF16),
        V((ZL, rows, CW), BF16), V((NS, rows, PC), BF16), V((NS, rows, PC), BF16),
        V((NZ, Y, rows, CW), BF16),
        V((L.ZH, Y * rows, L.HID), F32), V((L.ZH, Y * rows, L.HID), F32), V((L.ZH, Y * rows, L.HID), BF16),
        V((NZ, Y, rows, CW), BF16), V((NZ, rows, CW), BF16), V((NZ, 2, rows, CW), BF16),
        V((NZ, rows, CW), BF16), V((NZ, rows, CW), BF16),
        V((NZ * NXC, rows, PC), BF16), V((NS, rows, PC), BF16), V((rows, L.D), BF16),
        V((Y, 8, 128), F32), V((NZ, 8, 128), F32), V((L.X, 8, 128), F32), V((L.C, 8, 128), F32),
        dma, dma, dma, dma, dma, dma((NZ,)), dma, dma((NZ,)), dma((NZ,)), dma((NZ,)),
        dma, dma((NZ,)), dma((NZ,)), dma((NZ,)), dma, dma, dma, dma, dma((4,)), dma((4,)),
    ]
    return pl.pallas_call(
        functools.partial(kernel, L, tokens),
        out_shape=(
            jax.ShapeDtypeStruct((EXP_DEV,), F32),
            jax.ShapeDtypeStruct((EXP_DEV,), F32),
            jax.ShapeDtypeStruct((rows, L.D), BF16),
        ),
        in_specs=[smem, smem, smem, vmem, vmem, anyspace, anyspace, anyspace, anyspace],
        out_specs=(smem, smem, anyspace),
        scratch_shapes=scratch,
        compiler_params=pltpu.CompilerParams(
            collective_id=0, has_side_effects=True, vmem_limit_bytes=60 * 1024 * 1024
        ),
        name="probe_pass",
    )(
        targets, sources, probe_ids, expert_ids.T, norm_gain.reshape(L.D // 128, 128),
        routed, gate_weight[0], up_weight[0], down_weight[0],
    )


def build(mesh, L, tokens):
    both = ("dp", "expert")
    return jax.shard_map(
        functools.partial(on_device, L, tokens),
        mesh=mesh,
        in_specs=(
            P(both, None), P(both, None), P(), P("expert", None, "dp"), P("expert", None, "dp"),
            P("expert", "dp", None), P(), P(), P(both),
        ),
        out_specs=(P("expert"), P("expert"), P(both, None)),
        check_vma=False,
    )


def solution(mesh):
    L = Layout()
    return build(mesh, L, L.TOKS * L.ZH * L.Y * L.NS)
```

time: 355 us -> 143 us (0.40)
  waiting for transfers between devices: 253 us -> 0 us
  Pallas kernels: 0 us -> 135 us
  starting transfers between devices: 36.4 us -> 0 us
  blocking collectives: 21.7 us -> 0 us
  between operations: 14 us -> 0.64 us
  local copies, waits for them, and re-layouts: 15.6 us -> 4.15 us
  matrix products: 7.84 us -> 0 us
  other arithmetic: 6.51 us -> 1.38 us
    pallas_call x0 -> x1, Pallas kernels: none -> 135 us  [on_device(): pl.pallas_call(functools.partial(kernel, L, tokens), out_shape=(jax.Shape...]
    all_gather x1 -> x0, waiting for transfers between devices: 103 us -> none  [expert_block(): piece = lax.all_gather(normed, DP, axis=0, tiled=True)]
    reduce_scatter x2 -> x0, waiting for transfers between devices: 89.9 us -> none  [own_block(): blocks = lax.psum_scatter(blocks, axes[k], scatter_dimension=0, tiled=True)]
    all_to_all x5 -> x0, waiting for transfers between devices: 59.7 us -> none  [the longest x2 35.1 us: relay_rows(): lax.all_to_all(shaped, 'expert', split_axis=0, concat_axis=0, tiled=True)]
    all_to_all x5 -> x0, starting transfers between devices: 36.3 us -> none  [the longest x2 16.8 us: relay_rows(): lax.all_to_all(shaped, 'expert', split_axis=0, concat_axis=0, tiled=True)]
    all_to_all x1 -> x0, blocking collectives: 21.7 us -> none  [relay_rows(): lax.all_to_all(jnp.take(lax.all_to_all(shaped, 'expert', split_axis=0, co...]
    dot_general x4 -> x0, matrix products: 7.84 us -> none  [the longest x1 4.91 us: expert_block(): gate_value = jnp.dot(piece, gate_matrix, preferred_element_type=jnp.float32)]
    reshape x3 -> x0, local copies, waits for them, and re-layouts: 5.55 us -> none  [the longest x2 2.9 us: relay_rows(): return moved.reshape(array.shape)]
  transfers between devices with their start and end apart: 8 -> 0, of which waited for: 7 -> 0; matrix products, arithmetic and copies ran while one was open for 2% -> 0% of each run, Pallas kernels for 0% -> 0%
where the time goes in v1:
time: 143 us; the launch traced here: 141 us
  Pallas kernels  135 us (94%)
  local copies, waits for them, and re-layouts  4.15 us (3%)
    pallas_call x1, Pallas kernels, on_device(): pl.pallas_call(functools.partial(kernel, L, tokens), out_shape=(jax.Shape...  135 us
    unnamed x3, local copies, waits for them, and re-layouts  4.15 us

profile of v1, /device:TPU:1, one launch (start us, length us, event | category | flops | bytes accessed | tf_op | source)
XLA Modules:
  0.0 141.0 jit_solution(2678797062798060655)
XLA Ops:
  0.6 1.4 fusion.1
  2.0 134.8 %probe_pass.1 = (f32[8]{0:T(128)}, f32[8]{0:T(128)}, bf16[40,7168]{1,0:T(8,128)(2,1)}) custom-call(s32[32]{0:T(128)} %get-tuple-element.4.tgt_ref, s32[32]{0:T(128)} %get-tuple-element.3.src_ref, s32[40]{0:T(128)} %pid_ref.1, s32[8,128]{1,0:T(8,128)} %bitcast.9, bf16[56,128]{1,0:T(8,128)(2,1)} %bitcast.8, bf16[128,7168]{1,0:T(8,128)(2,1)} %routed_hbm.1, ...), custom_call_target="tpu_custom_call" | custom-call | tf_op jit(solution)/shard_map/probe_pass/pallas_call | solution.py:432
  136.9 1.1 copy.15
  138.0 1.1 copy.16
  139.1 1.9 %copy.17 = bf16[40,7168]{1,0:T(8,128)(2,1)} copy(bf16[40,7168]{1,0:T(8,128)(2,1)} %get-tuple-element.10) | data formatting | bytes 1146880

commit v2 on v1

v2 whole, which is shorter than its diff:
```python
import functools

import jax
import jax.numpy as jnp
from jax import lax
from jax.experimental import pallas as pl
from jax.experimental.pallas import tpu as pltpu
from jax.sharding import PartitionSpec as P

MESH = pl.DeviceIdType.MESH
F32 = jnp.float32
BF16 = jnp.bfloat16
EXP_DEV = 8
TOP = 8
EPS = 1e-06
PC = 256
LAG = 3
BACK_LAG = 3
LAST_LAG = 2


class Layout:
    def __init__(self, zh=2, y=4, zl=4, x=4, c=2, pieces=7, rows=40, toks=128, hid=256):
        self.ZH, self.Y, self.ZL, self.X, self.C = zh, y, zl, x, c
        self.KP, self.ROWS, self.TOKS, self.HID = pieces, rows, toks, hid
        self.NZ, self.NXC = zh * zl, x * c
        self.NS = zl * x * c
        self.CW = pieces * PC
        self.D = zl * self.CW
        head = rows * 2 // 5 // 8 * 8 or rows // 2
        self.PARTS = ((0, head), (head, rows - head))


def kernel(
    L, tokens,
    old_ref, new_ref, pid_ref, ids_ref, gain_ref, routed_hbm, gate_hbm, up_hbm, down_hbm,
    stats_hbm, out_hbm,
    routed_v, gain_v, gate_v, up_v, down_v,
    send1, recv1_a, recv1_b, send2_a, send2_b, xbuf, gacc, uacc, hid,
    pbuf, ra, rb, bs, sz, zr_a, zr_b, f1_a, f1_b, fin,
    st_y, st_z, st_x, st_c, st_out, tgt_ref, src_ref,
    in_sem, w_sem, s1_send, s1_recv, s2_send, s2_recv, y_send, yp_recv, ym_recv, yf_recv,
    r_send, ra_recv, rb0_recv, rb1_recv, z_send, zr_recv, f_send, f_recv, st_send, st_recv, st_sem,
):
    Y, ZL, X, C, KP, NZ, NXC, NS, CW = L.Y, L.ZL, L.X, L.C, L.KP, L.NZ, L.NXC, L.NS, L.CW
    rows = L.ROWS
    PARTS = L.PARTS
    recv1, send2, zr, f1 = (recv1_a, recv1_b), (send2_a, send2_b), (zr_a, zr_b), (f1_a, f1_b)
    me_d, me_e = lax.axis_index("dp"), lax.axis_index("expert")
    div, rem = lax.div, lax.rem
    zh, y = div(me_d, Y), rem(me_d, Y)
    zl, xc = div(me_e, NXC), rem(me_e, NXC)
    x, c = div(xc, C), rem(xc, C)
    p = zh * ZL + zl
    kme = rem(xc - C * zl + C * NXC, NXC)
    active = kme < KP
    mine = p * NXC + xc
    offs = [((t + 1) // 2) * (2 * (t % 2) - 1) for t in range(NZ)]
    REACH = ZL // 2
    zs = [rem(p + o + NZ, NZ) for o in offs]
    xcs = [rem(xc + q, NXC) for q in range(NXC)]

    def dev(z, yy, xcc):
        return (div(z, ZL) * Y + yy, rem(z, ZL) * NXC + xcc)

    def half(r, z_low):
        return div(rem(r - z_low + ZL // 2 - 1 + rem(r, 2) + NZ, NZ), ZL)

    def span(part):
        return pl.ds(*PARTS[part])

    def cols(k):
        return pl.ds(pl.multiple_of(k * PC, PC), PC)

    def remote(src, dst, send, recv, where):
        pltpu.make_async_remote_copy(
            src_ref=src, dst_ref=dst, send_sem=send, recv_sem=recv, device_id=where, device_id_type=MESH
        ).start()

    def wait(ref, sem):
        pltpu.make_async_copy(ref, ref, sem).wait()

    copy_in = pltpu.make_async_copy(routed_hbm, routed_v, in_sem)
    copy_in.start()
    barrier = pltpu.get_barrier_semaphore()

    for t in reversed(range(NZ)):
        for q in reversed(range(NXC)):
            if (t or q) and abs(offs[t]) <= REACH:
                pl.semaphore_signal(barrier, inc=1, device_id=dev(zs[t], y, xcs[q]), device_id_type=MESH)
    for dy in range(1, Y):
        pl.semaphore_signal(barrier, inc=1, device_id=dev(p, rem(y + dy, Y), xc), device_id_type=MESH)

    gain_v[...] = gain_ref[...].astype(F32)
    lane = lax.broadcasted_iota(jnp.int32, (8, L.TOKS), 1)
    sub = lax.broadcasted_iota(jnp.int32, (8, L.TOKS), 0)
    picks = []
    for b in range(rows // 8):
        want = jnp.zeros((8, L.TOKS), jnp.int32)
        for i in range(8):
            want = jnp.where(sub == i, pid_ref[b * 8 + i], want)
        picks.append((lane == want).astype(F32))
    select = jnp.concatenate(picks, axis=0).astype(BF16)

    copy_in.wait()
    for hbm, v in ((gate_hbm, gate_v), (up_hbm, up_v)):
        for m in range(ZL):
            pltpu.make_async_copy(hbm.at[pl.ds(m * CW, CW), :], v.at[m], w_sem).start()
    for m in range(ZL):
        pltpu.make_async_copy(down_hbm.at[:, pl.ds(m * CW, CW)], down_v.at[m], w_sem).start()

    square = jnp.zeros((rows, 1), F32)
    for m in range(ZL):
        picked = jnp.dot(select, routed_v[:, m * CW : (m + 1) * CW], preferred_element_type=F32)
        square += jnp.sum(picked * picked, axis=1, keepdims=True)
        send1[m] = picked.astype(BF16)
    scale = lax.rsqrt(square / L.D + EPS)
    for m in range(ZL):
        for t in range(CW // 128):
            tile = m * (CW // 128) + t
            v = send1[m, :, t * 128 : (t + 1) * 128].astype(F32)
            send1[m, :, t * 128 : (t + 1) * 128] = (v * scale * gain_v[tile : tile + 1, :]).astype(BF16)

    pl.semaphore_wait(barrier, sum(abs(o) <= REACH for o in offs) * NXC - 1 + Y - 1)

    near = [(m, m + ZL * rem(half(m, zl) + zh, 2)) for m in range(ZL)]
    def to_relays(part):
        for n in range(KP):
            k = rem(xc + n, KP)
            for m, r in near:
                xct = rem(k + C * m, NXC)

                @pl.when(r * NXC + xct != mine)
                def _():
                    remote(
                        send1.at[m, span(part), cols(k)], recv1[part].at[me_e], s1_send, s1_recv.at[part],
                        dev(r, y, xct),
                    )

    to_relays(0)

    def find(out, values, among):
        @pl.loop(0, NS)
        def _(i):
            value = values[i]
            found = 0
            for j in range(NS):
                found = jnp.where(among[j] == value, j, found)
            out[i] = found

    find(tgt_ref, old_ref, new_ref)
    find(src_ref, new_ref, old_ref)

    def squares(i, acc):
        v = routed_v[:, pl.ds(pl.multiple_of(i * PC, PC), PC)].astype(F32)
        return acc + v * v

    total = lax.fori_loop(0, L.D // PC, squares, jnp.zeros((L.TOKS, PC), F32))
    mean_square = jnp.sum(total, axis=1, keepdims=True) / L.D
    ids = ids_ref[...].astype(F32).T
    expert = lax.broadcasted_iota(jnp.int32, (L.TOKS, 256), 1).astype(F32)
    onehot = jnp.zeros((L.TOKS, 256), F32)
    for k in range(TOP):
        onehot += (ids[:, k : k + 1] == expert).astype(F32)
    counts = jnp.sum(onehot, axis=0, keepdims=True)
    energy = jnp.sum(onehot * mean_square, axis=0, keepdims=True)
    stats = jnp.concatenate(
        [counts[:, :128], counts[:, 128:], energy[:, :128], energy[:, 128:], jnp.zeros((4, 128), F32)], axis=0
    )
    rounds = (
        (st_y, Y, y, lambda o: dev(p, o, xc)),
        (st_z, NZ, p, lambda o: dev(o, y, xc)),
        (st_x, X, x, lambda o: dev(p, y, o * C + c)),
        (st_c, C, c, lambda o: dev(p, y, x * C + o)),
    )

    def stats_store(n, value):
        buf, _, own, _ = rounds[n]
        buf[own] = value

    def stats_send(n):
        buf, size, own, where = rounds[n]
        for step in range(1, size):
            remote(buf.at[own], buf.at[own], st_send.at[n], st_recv.at[n], where(rem(own + step, size)))

    def stats_sum(n):
        buf, size, own, _ = rounds[n]
        if size > 1:
            wait(buf.at[pl.ds(0, size - 1)], st_recv.at[n])
            wait(buf.at[pl.ds(0, size - 1)], st_send.at[n])
        value = buf[0]
        for o in range(1, size):
            value += buf[o]
        return value

    def stats_out(value):
        where = lax.broadcasted_iota(jnp.int32, (2, 128), 0) * 128 + lax.broadcasted_iota(jnp.int32, (2, 128), 1)
        row, col = lax.broadcasted_iota(jnp.int32, (8, 128), 0), lax.broadcasted_iota(jnp.int32, (8, 128), 1)
        tile = jnp.zeros((8, 128), F32)
        for i in range(EXP_DEV):
            hit = where == me_e * EXP_DEV + i
            for n in range(2):
                one = jnp.sum(jnp.where(hit, value[2 * n : 2 * n + 2], 0.0))
                tile = jnp.where((row == n) & (col == i), one, tile)
        st_out[...] = tile
        pltpu.make_async_copy(st_out, stats_hbm, st_sem).start()

    def stats_next(n):
        stats_store(n, stats_sum(n - 1))

    stats_store(0, stats)
    to_relays(1)

    def relay(part):
        @pl.when(active)
        def _():
            got, put = recv1[part], send2[part]
            got[me_e] = send1[zl, span(part), cols(kme)]
            wait(got.at[pl.ds(0, NS - 1)], s1_recv.at[part])
            for j in range(NS):
                put[j] = got[tgt_ref[j]]
            xbuf[p, y, span(part), cols(kme)] = got[tgt_ref[me_e]]

    def to_holders(part, ts):
        @pl.when(active)
        def _():
            for t in ts:
                for q in range(NXC):
                    if t or q:
                        remote(
                            send2[part].at[rem(zs[t], ZL) * NXC + xcs[q]],
                            xbuf.at[p, y, span(part), cols(kme)],
                            s2_send.at[part],
                            s2_recv.at[part * NZ + p],
                            dev(zs[t], y, xcs[q]),
                        )

    slot = tgt_ref[me_e]
    slot_z = div(slot, NXC)
    ynext, yprev, yopp = rem(y + 1, Y), rem(y + Y - 1, Y), rem(y + 2, Y)

    pairs = []
    for a in range(NZ):
        for b in range(a + 1, NZ):
            if (offs[a] - offs[b]) % NZ == ZL:
                pairs.append((b, a))
    pairs.sort()
    orders = (list(range(NZ)), [i for b, a in pairs[:-1] for i in (a, b)] + list(pairs[-1]))

    def place(u):
        return u // NZ, orders[u // NZ][u % NZ]

    def ring(i):
        return zs[i]

    def block(u, who):
        part, i = place(u)
        return xbuf.at[ring(i), who, span(part)]

    def own_group(u):
        part, i = place(u)
        mine_here = block(u, y)
        sem = s2_recv.at[part * NZ + ring(i)]
        if offs[i] == 0:
            @pl.when(active)
            def _():
                if KP > 1:
                    wait(xbuf.at[p, y, span(part), pl.ds(0, CW - PC)], sem)

            @pl.when(jnp.logical_not(active))
            def _():
                wait(mine_here, sem)
        else:
            wait(mine_here, sem)
        remote(mine_here, mine_here, y_send, yp_recv.at[u], dev(p, ynext, xc))
        remote(mine_here, mine_here, y_send, ym_recv.at[u], dev(p, yprev, xc))

    def forward(u):
        if u % 2 == 0:
            wait(block(u, yprev), yp_recv.at[u])
            remote(block(u, yprev), block(u, yprev), y_send, yf_recv.at[u], dev(p, ynext, xc))
        else:
            wait(block(u, ynext), ym_recv.at[u])
            remote(block(u, ynext), block(u, ynext), y_send, yf_recv.at[u], dev(p, yprev, xc))

    def arrived(u):
        if u % 2 == 0:
            wait(block(u, ynext), ym_recv.at[u])
        else:
            wait(block(u, yprev), yp_recv.at[u])
        wait(block(u, yopp), yf_recv.at[u])

    first = [True]

    def project(a, b):
        for i in (a, b):
            arrived(i)
            arrived(NZ + orders[1].index(i))
        m = rem(ring(a), ZL)
        near = half(m, slot_z) == 0
        lhs = jnp.concatenate([xbuf[m].reshape(Y * rows, CW), xbuf[m + ZL].reshape(Y * rows, CW)], axis=0)
        opening = first[0]
        first[0] = False
        if opening:
            wait(gate_v, w_sem)
            wait(up_v, w_sem)
            wait(down_v, w_sem)
        for weight, acc in ((gate_v, gacc), (up_v, uacc)):
            value = jnp.dot(lhs, weight[m], preferred_element_type=F32)
            a, b = value[: Y * rows], value[Y * rows :]
            for h, part in ((0, jnp.where(near, a, b)), (1, jnp.where(near, b, a))):
                if opening:
                    acc[h] = part
                else:
                    acc[h] += part

    units = 2 * NZ
    relay(0)
    to_holders(0, range(NZ))
    stats_send(0)
    own_group(0)
    relay(1)
    to_holders(1, orders[1][: NZ // 2])
    for u in range(1, units):
        own_group(u)
        if u - 1 in range(NZ // 2):
            to_holders(1, orders[1][NZ // 2 + u - 1 : NZ // 2 + u])
        if u >= LAG:
            forward(u - LAG)
        if u == units // 4:
            stats_next(1)
        if u == units // 4 + 1:
            stats_send(1)
        if u == units - 3:
            stats_next(2)
        if u == units - 2:
            stats_send(2)
    for u in range(units - LAG, units):
        forward(u)
        if u < units - 1 and len(pairs) > 2:
            project(*pairs.pop(0)[::-1])
    for b, a in pairs:
        project(a, b)

    g = gacc[...]
    hid[...] = (g / (1.0 + jnp.exp(-g)) * uacc[...]).astype(BF16)

    def back(i):
        return ring(NZ - 1 - i)

    def sign(i):
        return (ynext, yprev) if i % 2 == 0 else (yprev, ynext)

    def compute(i):
        r = back(i)
        value = jnp.dot(hid[half(r, slot_z)], down_v[rem(r, ZL)], preferred_element_type=F32)
        pbuf[i] = value.astype(BF16).reshape(Y, rows, CW)

    def unit(v):
        return 1 - v // NZ, v % NZ

    def send_parts(v):
        part, i = unit(v)
        to, _ = sign(v)
        remote(pbuf.at[i, yopp, span(part)], ra.at[i, span(part)], r_send, ra_recv.at[v], dev(p, to, xc))

    def add_passing(v):
        part, i = unit(v)
        to, _ = sign(v)
        wait(ra.at[i, span(part)], ra_recv.at[v])
        bs[i, span(part)] = (pbuf[i, to, span(part)].astype(F32) + ra[i, span(part)].astype(F32)).astype(BF16)

    def send_passing(v):
        part, i = unit(v)
        to, other = sign(v)
        remote(bs.at[i, span(part)], rb.at[i, 1, span(part)], r_send, rb1_recv.at[v], dev(p, to, xc))
        remote(pbuf.at[i, other, span(part)], rb.at[i, 0, span(part)], r_send, rb0_recv.at[v], dev(p, other, xc))

    def add_own(v):
        part, i = unit(v)
        rw = span(part)
        wait(rb.at[i, 0, rw], rb0_recv.at[v])
        wait(rb.at[i, 1, rw], rb1_recv.at[v])
        sz[i, rw] = (pbuf[i, y, rw].astype(F32) + rb[i, 0, rw].astype(F32) + rb[i, 1, rw].astype(F32)).astype(BF16)

    def send_relays(v):
        part, i = unit(v)
        r = back(i)
        m = rem(r, ZL)
        for n in range(KP):
            k = rem(xc + n, KP)
            xct = rem(k + C * m, NXC)

            def go():
                remote(
                    sz.at[i, span(part), cols(k)], zr[part].at[mine], z_send.at[part], zr_recv.at[part], dev(r, y, xct)
                )

            if offs[NZ - 1 - i] == 0:
                pl.when(xct != xc)(go)
            else:
                go()

    chunk = pl.ds(pl.multiple_of(zl * CW + kme * PC, PC), PC)

    def relay_back(part):
        @pl.when(active)
        def _():
            got, put = zr[part], f1[part]
            got[mine] = sz[NZ - 1, span(part), cols(kme)]
            wait(got.at[pl.ds(0, NZ * NXC - 1)], zr_recv.at[part])
            for s in range(NS):
                j = src_ref[s]
                put[s] = (got[j].astype(F32) + got[j + NS].astype(F32)).astype(BF16)
            fin[span(part), chunk] = put[me_e]

            for n in range(ZL):
                s_z = rem(zl + n, ZL)
                z = ZL * half(p, s_z) + s_z
                for q in range(NXC):
                    if n or q:
                        remote(
                            put.at[s_z * NXC + xcs[q]], fin.at[span(part), chunk], f_send.at[part], f_recv.at[part],
                            dev(z, y, xcs[q]),
                        )

    compute(0)
    for v in range(units + BACK_LAG + LAST_LAG):
        if v < units:
            send_parts(v)
        passing = v - BACK_LAG
        if 0 <= passing < units:
            add_passing(passing)
        if v + 1 < NZ:
            compute(v + 1)
        if 0 <= passing < units:
            send_passing(passing)
        done = v - BACK_LAG - LAST_LAG
        if done >= 0:
            add_own(done)
            if done == 2:
                stats_next(3)
            if done == 3:
                stats_send(3)
            if done == NZ + 1:
                stats_out(stats_sum(3))
            send_relays(done)
            if done == NZ + 3:
                relay_back(1)
    relay_back(0)

    def returned(part):
        @pl.when(active)
        def _():
            wait(send2[part].at[pl.ds(0, ZL * KP - 1)], f_recv.at[part])

        @pl.when(jnp.logical_not(active))
        def _():
            wait(send2[part].at[pl.ds(0, ZL * KP)], f_recv.at[part])

    returned(1)
    returned(0)
    copy_out = pltpu.make_async_copy(fin, out_hbm, in_sem)
    copy_out.start()

    @pl.when(active)
    def _():
        wait(send1.at[pl.ds(0, ZL - 1)], s1_send)
        if KP > 1:
            wait(send1.at[0, :, pl.ds(0, CW - PC)], s1_send)
        for part in range(2):
            wait(zr[part].at[pl.ds(0, NZ * NXC - 1)], s2_send.at[part])
            wait(zr[part].at[pl.ds(0, NZ * KP - 1)], z_send.at[part])
            wait(zr[part].at[pl.ds(0, NS - 1)], f_send.at[part])

    @pl.when(jnp.logical_not(active))
    def _():
        wait(send1, s1_send)
        for part in range(2):
            wait(zr[part].at[pl.ds(0, NZ * KP)], z_send.at[part])

    wait(pbuf.at[pl.ds(0, 3 * NZ // Y)], y_send)
    wait(pbuf.at[pl.ds(0, 3 * NZ // Y)], r_send)
    pltpu.make_async_copy(st_out, stats_hbm, st_sem).wait()
    copy_out.wait()


def on_device(L, tokens, routed, expert_ids, norm_gain, gate_weight, up_weight, down_weight, old_place, new_place, probe_ids):
    NZ, NXC, Y, ZL, KP, NS, CW, rows = L.NZ, L.NXC, L.Y, L.ZL, L.KP, L.NS, L.CW, L.ROWS
    smem = pl.BlockSpec(memory_space=pltpu.SMEM)
    vmem = pl.BlockSpec(memory_space=pltpu.VMEM)
    anyspace = pl.BlockSpec(memory_space=pl.ANY)
    dma = pltpu.SemaphoreType.DMA
    V = pltpu.VMEM

    def pieces(n):
        return [V((n, size, PC), BF16) for _, size in L.PARTS]

    scratch = [
        V((L.TOKS, L.D), BF16), V((L.D // 128, 128), F32),
        V((ZL, CW, L.HID), BF16), V((ZL, CW, L.HID), BF16), V((ZL, L.HID, CW), BF16),
        V((ZL, rows, CW), BF16), *pieces(NS), *pieces(NS),
        V((NZ, Y, rows, CW), BF16),
        V((L.ZH, Y * rows, L.HID), F32), V((L.ZH, Y * rows, L.HID), F32), V((L.ZH, Y * rows, L.HID), BF16),
        V((NZ, Y, rows, CW), BF16), V((NZ, rows, CW), BF16), V((NZ, 2, rows, CW), BF16),
        V((NZ, rows, CW), BF16), V((NZ, rows, CW), BF16),
        *pieces(NZ * NXC), *pieces(NS), V((rows, L.D), BF16),
        V((Y, 8, 128), F32), V((NZ, 8, 128), F32), V((L.X, 8, 128), F32), V((L.C, 8, 128), F32), V((8, 128), F32),
        pltpu.SMEM((NS,), jnp.int32), pltpu.SMEM((NS,), jnp.int32),
        dma, dma, dma, dma((2,)), dma((2,)), dma((2 * NZ,)), dma, dma((2 * NZ,)), dma((2 * NZ,)), dma((2 * NZ,)),
        dma, dma((2 * NZ,)), dma((2 * NZ,)), dma((2 * NZ,)), dma((2,)), dma((2,)), dma((2,)), dma((2,)), dma((4,)), dma((4,)), dma,
    ]
    stats, probe_out = pl.pallas_call(
        functools.partial(kernel, L, tokens),
        out_shape=(
            jax.ShapeDtypeStruct((8, 128), F32),
            jax.ShapeDtypeStruct((rows, L.D), BF16),
        ),
        in_specs=[smem, smem, smem, vmem, vmem, anyspace, anyspace, anyspace, anyspace],
        out_specs=(anyspace, anyspace),
        scratch_shapes=scratch,
        compiler_params=pltpu.CompilerParams(
            collective_id=0, has_side_effects=True, vmem_limit_bytes=60 * 1024 * 1024
        ),
        name="probe_pass",
    )(
        old_place, new_place, probe_ids, expert_ids.T, norm_gain.reshape(L.D // 128, 128),
        routed, gate_weight[0], up_weight[0], down_weight[0],
    )
    counts, energy = stats[0, :EXP_DEV], stats[1, :EXP_DEV]
    return counts * (EXP_DEV * NS) / (tokens * TOP), energy / counts, probe_out


def build(mesh, L, tokens):
    both = ("dp", "expert")
    return jax.shard_map(
        functools.partial(on_device, L, tokens),
        mesh=mesh,
        in_specs=(
            P(both, None), P(both, None), P(), P("expert", None, "dp"), P("expert", None, "dp"),
            P("expert", "dp", None), P(), P(), P(both),
        ),
        out_specs=(P("expert"), P("expert"), P(both, None)),
        check_vma=False,
    )


def solution(mesh):
    L = Layout()
    return build(mesh, L, L.TOKS * L.ZH * L.Y * L.NS)
```

time: 143 us -> 129 us (0.902)
  Pallas kernels: 135 us -> 125 us
  local copies, waits for them, and re-layouts: 4.15 us -> 1.9 us
    pallas_call x1, Pallas kernels: 135 us -> 125 us  [on_device(): pl.pallas_call(functools.partial(kernel, L, tokens), out_shape=(jax.Shape...]
    unnamed x3 -> x1, local copies, waits for them, and re-layouts: 4.15 us -> 1.9 us
where the time goes in v2:
time: 129 us; the launch traced here: 128 us
  Pallas kernels  125 us (97%)
  local copies, waits for them, and re-layouts  1.9 us (1%)
    pallas_call x1, Pallas kernels, on_device(): pl.pallas_call(functools.partial(kernel, L, tokens), out_shape=(jax.Shape...  125 us

profile of v2, /device:TPU:1, one launch (start us, length us, event | category | flops | bytes accessed | tf_op | source)
XLA Modules:
  0.0 128.4 jit_solution(9766263240722994998)
XLA Ops:
  0.6 124.6 %probe_pass.1 = (f32[8,128]{1,0:T(8,128)}, bf16[40,7168]{1,0:T(8,128)(2,1)}) custom-call(s32[32]{0:T(128)} %old_ref.1, s32[32]{0:T(128)} %new_ref.1, s32[40]{0:T(128)} %pid_ref.1, s32[8,128]{1,0:T(8,128)} %bitcast.13, bf16[56,128]{1,0:T(8,128)(2,1)} %bitcast.12, bf16[128,7168]{1,0:T(8,128)(2,1)} %routed_hbm.1, bf16[7168,256]{1,0:T(8,128)(2,1)} %bitcast.9, ...), custom_call_target="tpu_custom_call" | custom-call | tf_op jit(solution)/shard_map/probe_pass/pallas_call | solution.py:513
  125.3 1.3 fusion
  126.5 1.9 %copy.13 = bf16[40,7168]{1,0:T(8,128)(2,1)} copy(bf16[40,7168]{1,0:T(8,128)(2,1)} %get-tuple-element.14) | data formatting | bytes 1146880

commit v3 on v2

--- a/solution.py
+++ b/solution.py
@@ -14,7 +14,7 @@
 TOP = 8
 EPS = 1e-06
 PC = 256
-LAG = 3
+LAG = 2
 BACK_LAG = 3
 LAST_LAG = 2
 
@@ -245,7 +245,7 @@
             if (offs[a] - offs[b]) % NZ == ZL:
                 pairs.append((b, a))
     pairs.sort()
-    orders = (list(range(NZ)), [i for b, a in pairs[:-1] for i in (a, b)] + list(pairs[-1]))
+    orders = (list(range(NZ)), list(range(NZ)))
 
     def place(u):
         return u // NZ, orders[u // NZ][u % NZ]

time: 129 us -> 125 us (0.969)
  Pallas kernels: 125 us -> 121 us
    pallas_call x1, Pallas kernels: 125 us -> 121 us  [on_device(): pl.pallas_call(functools.partial(kernel, L, tokens), out_shape=(jax.Shape...]
where the time goes in v3:
time: 125 us; the launch traced here: 124 us
  Pallas kernels  121 us (97%)
  local copies, waits for them, and re-layouts  1.9 us (2%)
  other arithmetic  1.27 us (1%)
    pallas_call x1, Pallas kernels, on_device(): pl.pallas_call(functools.partial(kernel, L, tokens), out_shape=(jax.Shape...  121 us

profile of v3, /device:TPU:1, one launch (start us, length us, event | category | flops | bytes accessed | tf_op | source)
XLA Modules:
  0.0 124.3 jit_solution(7570422077722826700)
XLA Ops:
  0.6 120.5 %probe_pass.1 = (f32[8,128]{1,0:T(8,128)}, bf16[40,7168]{1,0:T(8,128)(2,1)}) custom-call(s32[32]{0:T(128)} %old_ref.1, s32[32]{0:T(128)} %new_ref.1, s32[40]{0:T(128)} %pid_ref.1, s32[8,128]{1,0:T(8,128)} %bitcast.13, bf16[56,128]{1,0:T(8,128)(2,1)} %bitcast.12, bf16[128,7168]{1,0:T(8,128)(2,1)} %routed_hbm.1, bf16[7168,256]{1,0:T(8,128)(2,1)} %bitcast.9, ...), custom_call_target="tpu_custom_call" | custom-call | tf_op jit(solution)/shard_map/probe_pass/pallas_call | solution.py:513
  121.2 1.3 %fusion = (f32[8]{0:T(128)}, f32[8]{0:T(128)}) fusion(f32[8,128]{1,0:T(8,128)} %get-tuple-element.5), kind=kLoop, calls=%fused_computation.2 | loop fusion | flops 16 | bytes 128 | tf_op jit(solution)/shard_map/div | solution.py:531
  122.4 1.9 %copy.13 = bf16[40,7168]{1,0:T(8,128)(2,1)} copy(bf16[40,7168]{1,0:T(8,128)(2,1)} %get-tuple-element.14) | data formatting | bytes 1146880

commit v4 on v3

--- a/solution.py
+++ b/solution.py
@@ -39,8 +39,8 @@
     send1, recv1_a, recv1_b, send2_a, send2_b, xbuf, gacc, uacc, hid,
     pbuf, ra, rb, bs, sz, zr_a, zr_b, f1_a, f1_b, fin,
     st_y, st_z, st_x, st_c, st_out, tgt_ref, src_ref,
-    in_sem, w_sem, s1_send, s1_recv, s2_send, s2_recv, y_send, yp_recv, ym_recv, yf_recv,
-    r_send, ra_recv, rb0_recv, rb1_recv, z_send, zr_recv, f_send, f_recv, st_send, st_recv, st_sem,
+    in_sem, w_sem, s1_send, s1_recv, s2_send, s2_recv, y_send, y_recv, yf_recv,
+    r_send, ra_recv, rb0_recv, rb1_recv, z_send, zr_recv, f_send, f_recv, st_send, st_recv, st_sem, out_sem,
 ):
     Y, ZL, X, C, KP, NZ, NXC, NS, CW = L.Y, L.ZL, L.X, L.C, L.KP, L.NZ, L.NXC, L.NS, L.CW
     rows = L.ROWS
@@ -257,6 +257,8 @@
         part, i = place(u)
         return xbuf.at[ring(i), who, span(part)]
 
+    units = 2 * NZ
+
     def own_group(u):
         part, i = place(u)
         mine_here = block(u, y)
@@ -272,22 +274,18 @@
                 wait(mine_here, sem)
         else:
             wait(mine_here, sem)
-        remote(mine_here, mine_here, y_send, yp_recv.at[u], dev(p, ynext, xc))
-        remote(mine_here, mine_here, y_send, ym_recv.at[u], dev(p, yprev, xc))
+        remote(mine_here, mine_here, y_send, y_recv.at[u], dev(p, ynext, xc))
+        remote(mine_here, mine_here, y_send, y_recv.at[units + u], dev(p, yprev, xc))
 
     def forward(u):
-        if u % 2 == 0:
-            wait(block(u, yprev), yp_recv.at[u])
-            remote(block(u, yprev), block(u, yprev), y_send, yf_recv.at[u], dev(p, ynext, xc))
-        else:
-            wait(block(u, ynext), ym_recv.at[u])
-            remote(block(u, ynext), block(u, ynext), y_send, yf_recv.at[u], dev(p, yprev, xc))
+        way = rem(c + u, 2)
+        came = rem(y + Y - 1 + 2 * way, Y)
+        wait(block(u, came), y_recv.at[way * units + u])
+        remote(block(u, came), block(u, came), y_send, yf_recv.at[u], dev(p, rem(came + 2, Y), xc))
 
     def arrived(u):
-        if u % 2 == 0:
-            wait(block(u, ynext), ym_recv.at[u])
-        else:
-            wait(block(u, yprev), yp_recv.at[u])
+        way = 1 - rem(c + u, 2)
+        wait(block(u, rem(y + Y - 1 + 2 * way, Y)), y_recv.at[way * units + u])
         wait(block(u, yopp), yf_recv.at[u])
 
     first = [True]
@@ -314,7 +312,6 @@
                 else:
                     acc[h] += part
 
-    units = 2 * NZ
     relay(0)
     to_holders(0, range(NZ))
     stats_send(0)
@@ -348,8 +345,9 @@
     def back(i):
         return ring(NZ - 1 - i)
 
-    def sign(i):
-        return (ynext, yprev) if i % 2 == 0 else (yprev, ynext)
+    def sign(v):
+        to = rem(y + 1 + 2 * rem(c + v, 2), Y)
+        return to, rem(to + 2, Y)
 
     def compute(i):
         r = back(i)
@@ -458,10 +456,13 @@
         def _():
             wait(send2[part].at[pl.ds(0, ZL * KP)], f_recv.at[part])
 
+    def leave(part):
+        return pltpu.make_async_copy(fin.at[span(part)], out_hbm.at[span(part)], out_sem.at[part])
+
     returned(1)
+    leave(1).start()
     returned(0)
-    copy_out = pltpu.make_async_copy(fin, out_hbm, in_sem)
-    copy_out.start()
+    leave(0).start()
 
     @pl.when(active)
     def _():
@@ -482,7 +483,8 @@
     wait(pbuf.at[pl.ds(0, 3 * NZ // Y)], y_send)
     wait(pbuf.at[pl.ds(0, 3 * NZ // Y)], r_send)
     pltpu.make_async_copy(st_out, stats_hbm, st_sem).wait()
-    copy_out.wait()
+    for part in range(2):
+        leave(part).wait()
 
 
 def on_device(L, tokens, routed, expert_ids, norm_gain, gate_weight, up_weight, down_weight, old_place, new_place, probe_ids):
@@ -507,8 +509,8 @@
         *pieces(NZ * NXC), *pieces(NS), V((rows, L.D), BF16),
         V((Y, 8, 128), F32), V((NZ, 8, 128), F32), V((L.X, 8, 128), F32), V((L.C, 8, 128), F32), V((8, 128), F32),
         pltpu.SMEM((NS,), jnp.int32), pltpu.SMEM((NS,), jnp.int32),
-        dma, dma, dma, dma((2,)), dma((2,)), dma((2 * NZ,)), dma, dma((2 * NZ,)), dma((2 * NZ,)), dma((2 * NZ,)),
-        dma, dma((2 * NZ,)), dma((2 * NZ,)), dma((2 * NZ,)), dma((2,)), dma((2,)), dma((2,)), dma((2,)), dma((4,)), dma((4,)), dma,
+        dma, dma, dma, dma((2,)), dma((2,)), dma((2 * NZ,)), dma, dma((4 * NZ,)), dma((2 * NZ,)),
+        dma, dma((2 * NZ,)), dma((2 * NZ,)), dma((2 * NZ,)), dma((2,)), dma((2,)), dma((2,)), dma((2,)), dma((4,)), dma((4,)), dma, dma((2,)),
     ]
     stats, probe_out = pl.pallas_call(
         functools.partial(kernel, L, tokens),

time: 125 us -> 124 us (level)
  no operation moved by 1% of the time
where the time goes in v4:
time: 124 us
  Pallas kernels  120 us (97%)
  local copies, waits for them, and re-layouts  1.9 us (2%)
  other arithmetic  1.27 us (1%)
    pallas_call x1, Pallas kernels, on_device(): pl.pallas_call(functools.partial(kernel, L, tokens), out_shape=(jax.Shape...  120 us

profile of v4, /device:TPU:1, one launch (start us, length us, event | category | flops | bytes accessed | tf_op | source)
XLA Modules:
  0.0 124.2 jit_solution(1329282249076814523)
XLA Ops:
  0.6 120.4 %probe_pass.1 = (f32[8,128]{1,0:T(8,128)}, bf16[40,7168]{1,0:T(8,128)(2,1)}) custom-call(s32[32]{0:T(128)} %old_ref.1, s32[32]{0:T(128)} %new_ref.1, s32[40]{0:T(128)} %pid_ref.1, s32[8,128]{1,0:T(8,128)} %bitcast.13, bf16[56,128]{1,0:T(8,128)(2,1)} %bitcast.12, bf16[128,7168]{1,0:T(8,128)(2,1)} %routed_hbm.1, bf16[7168,256]{1,0:T(8,128)(2,1)} %bitcast.9, ...), custom_call_target="tpu_custom_call" | custom-call | tf_op jit(solution)/shard_map/probe_pass/pallas_call | solution.py:515
  121.0 1.3 %fusion = (f32[8]{0:T(128)}, f32[8]{0:T(128)}) fusion(f32[8,128]{1,0:T(8,128)} %get-tuple-element.5), kind=kLoop, calls=%fused_computation.2 | loop fusion | flops 16 | bytes 128 | tf_op jit(solution)/shard_map/div | solution.py:533
  122.3 1.9 %copy.13 = bf16[40,7168]{1,0:T(8,128)(2,1)} copy(bf16[40,7168]{1,0:T(8,128)(2,1)} %get-tuple-element.14) | data formatting | bytes 1146880
